TPU v7x, 128 devices: a whole 4x4x4 slice. The times are simulated.
128 devices in a mesh: gy: 16 (over z, x), gx: 8 (over y, core).
Axes of the slice: x: 4, y: 4, z: 4, core: 2. Of those that a mesh axis runs over, the one named last changes fastest.
Arguments:
- ensemble: bfloat16 [32, 2, 1024, 1024], P(None, None, 'gy', 'gx'), may hold values from -1.1953125 to 1.1953125
- obs_cell: int32 [16, 8, 2048], P('gy', 'gx'), may hold values from 0 to 8191
- obs_level: int32 [16, 8, 2048], P('gy', 'gx'), may hold values from 0 to 1
- innovation: float32 [16, 8, 2048], P('gy', 'gx'), may hold values from -6 to 6
- obs_weight: float32 [16, 8, 2048], P('gy', 'gx'), may hold values from 0.5 to 4
Outputs:
- control: float32 [32, 2, 1024, 1024], P(None, None, 'gy', 'gx')
- increment: float32 [2, 1024, 1024], P(None, 'gy', 'gx')
Inputs may be any that keep to these rules, and one draw needn't show every extreme that they name: obs_cell holds row * 128 + column of the observation within its device's block of 64 x 128 cells.
All inputs are finite; a program needn't handle non-finite values.
Results may differ from a plain program's by a relative error of at most 0.0003.
Values sent between devices are 32-bit elements; how exact they have to be, the bound alone decides.
A program may use at most 128 MiB of HBM per device.

v0:
```python
import jax
import jax.numpy as jnp
from jax import lax
from jax.experimental import pallas as pl
from jax.experimental.pallas import tpu as pltpu
from jax.sharding import PartitionSpec as P

MESH = pl.DeviceIdType.MESH
F32 = jnp.float32
BF16 = jnp.bfloat16
EPS = 1e-06
FILTER_SCALE = 0.2**4
MEMBERS = 32
LEVELS = 2
ROWS = 64
COLS = 128
HALO = 8
EROWS = ROWS + 2 * HALO
ECOLS = COLS + 2 * HALO
NR = EROWS // 8
NT = ECOLS // 8
CHUNKS = 4
PER = 16
OBS_STEP = 512

WAYS = ((-1, 0), (1, 0), (0, -1), (0, 1), (-1, -1), (-1, 1), (1, -1), (1, 1))


def total(values):
    while len(values) > 1:
        odd = values[len(values) - len(values) % 2 :]
        values = [a + b for a, b in zip(values[0::2], values[1::2])] + odd
    return values[0]


def by_rows(ref, *lead):
    return [ref[(*lead, pl.ds(r, 8, stride=NR), slice(None))] for r in range(NR)]


def put_rows(ref, values, *lead):
    for r in range(NR):
        ref[(*lead, pl.ds(r, 8, stride=NR), slice(None))] = values[r]


def tiles(ref, *lead):
    return [ref[(*lead, slice(8 * r, 8 * r + 8), slice(None))] for r in range(NR)]


def put_tiles(ref, values, *lead):
    for r in range(NR):
        ref[(*lead, slice(8 * r, 8 * r + 8), slice(None))] = values[r]


def sweep(load, store, masks):
    north, south, west, east = masks
    for first, last in ((0, NT // 2), (NT // 2, NT)):
        seen = {}

        def f(r, t):
            if (r, t) not in seen:
                if t == -1:
                    value = pltpu.roll(f(r, NT - 1), 1, 0)
                elif t == NT:
                    value = pltpu.roll(f(r, 0), 7, 0)
                elif r == -1:
                    value = pltpu.roll(f(NR - 1, t), 1, 1)
                elif r == NR:
                    value = pltpu.roll(f(0, t), 127, 1)
                else:
                    value = load(r, t)
                seen[r, t] = value
            return seen[r, t]

        def pair_row(r):
            return {t: f(r, t) + f(r + 1, t - 1) for t in range(first, last + 1)}

        def finish(r, above, here):
            for t in range(first, last):
                out = f(r, t) + (above[t] + here[t + 1])
                if r == 7:
                    out = out * north
                if r == 2:
                    out = out * south
                if t == 7:
                    out = out * west
                if t == 10:
                    out = out * east
                store(r, t, out)

        start = above = pair_row(0)
        for r in range(1, NR):
            here = pair_row(r)
            finish(r, above, here)
            above = here
        finish(0, pair_row(-1), start)


def kernel(
    n_gy,
    n_gx,
    ens,
    cell,
    level,
    innov,
    weight,
    control,
    increment,
    xin,
    cin,
    lin,
    iin,
    win,
    ext,
    xt,
    gt,
    sext,
    spk,
    sst,
    dext,
    grid,
    work,
    ft,
    acc,
    squares,
    image,
    rowa,
    rowb,
    staged,
    sinc,
    in_sem,
    xsend,
    xrecv,
    ssend,
    srecv,
    asend,
    arecv,
    bsend,
    brecv,
    out_sem,
):
    gy = lax.axis_index("gy")
    gx = lax.axis_index("gx")
    lane = lax.broadcasted_iota(jnp.int32, (8, 128), 1)
    sub = lax.broadcasted_iota(jnp.int32, (8, 128), 0)
    block = lane & 7

    loads = [
        pltpu.make_async_copy(src, dst, in_sem.at[i])
        for i, (src, dst) in enumerate(((ens, xin), (cell, cin), (level, lin), (innov, iin), (weight, win)))
    ]
    for load in loads:
        load.start()

    def there(dy, dx):
        return (lax.rem(gy + dy + n_gy, n_gy), lax.rem(gx + dx + n_gx, n_gx))

    def remote(src, dst, send, recv, to):
        return pltpu.make_async_remote_copy(
            src_ref=src, dst_ref=dst, send_sem=send, recv_sem=recv, device_id=to, device_id_type=MESH
        )

    barrier = pltpu.get_barrier_semaphore()
    met = [(0, k) for k in range(1, n_gx)] + [(k, 0) for k in range(1, n_gy)] + list(WAYS[4:])
    for dy, dx in met:
        pl.semaphore_signal(barrier, inc=1, device_id=there(dy, dx), device_id_type=MESH)

    loads[0].wait()

    def widen(i, carry):
        for k in range(4):
            ext[4 * i + k, HALO : HALO + ROWS, :] = xin[4 * i + k].astype(F32)
        return carry

    lax.fori_loop(0, MEMBERS * LEVELS // 4, widen, 0)

    def row_messages(c):
        fields = ext.at[pl.ds(c * PER, PER)]
        return [
            remote(fields.at[:, pl.ds(src, HALO), :], fields.at[:, pl.ds(dst, HALO), :], xsend.at[c, way], xrecv.at[c, way], there(*WAYS[way]))
            for way, (src, dst) in enumerate(((HALO, HALO + ROWS), (ROWS, 0)))
        ]

    def column_messages(c):
        fields = xt.at[c]
        return [
            remote(fields.at[:, pl.ds(src, HALO), :], fields.at[:, pl.ds(dst, HALO), :], xsend.at[c, way], xrecv.at[c, way], there(*WAYS[way]))
            for way, (src, dst) in ((2, (HALO, HALO + COLS)), (3, (COLS, 0)))
        ]

    pl.semaphore_wait(barrier, len(met))
    for c in range(CHUNKS):
        for msg in row_messages(c):
            msg.start()

    for load in loads[1:]:
        load.wait()
    grid[...] = jnp.zeros_like(grid)

    def scatter(k, carry):
        part = pl.ds(pl.multiple_of(k * OBS_STEP, OBS_STEP), OBS_STEP)
        where_at = cin[0, :, part]
        row = where_at >> 7
        col = (where_at & 127) + lin[0, :, part] * COLS
        w = win[0, :, part]
        on_row = lax.broadcasted_iota(jnp.int32, (ROWS, OBS_STEP), 0) == row
        on_col = lax.broadcasted_iota(jnp.int32, (LEVELS * COLS, OBS_STEP), 0) == col
        right = jnp.where(on_col, 1.0, 0.0).astype(BF16)
        left = []
        for value in (w * iin[0, :, part], w):
            for _ in range(3):
                piece = value.astype(BF16).astype(F32)
                left.append(jnp.where(on_row, piece, 0.0).astype(BF16))
                value = value - piece
        left = jnp.concatenate(left, axis=0)
        grid[...] += lax.dot_general(left, right, (((1,), (1,)), ((), ())), preferred_element_type=F32)
        return carry

    lax.fori_loop(0, cin.shape[-1] // OBS_STEP, scatter, 0)
    for lev in range(LEVELS):
        cols = slice(lev * COLS, lev * COLS + COLS)
        grad = grid[0:64, cols] + (grid[64:128, cols] + grid[128:192, cols])
        diag = grid[192:256, cols] + (grid[256:320, cols] + grid[320:384, cols])
        sext[0, lev, HALO : HALO + ROWS, :] = grad * FILTER_SCALE
        dext[lev, 0:HALO, :] = jnp.zeros((HALO, COLS), F32)
        dext[lev, HALO : HALO + ROWS, :] = diag
        dext[lev, HALO + ROWS : EROWS, :] = jnp.zeros((HALO, COLS), F32)

    def state_messages(kind):
        wide, west, east = sext.at[kind], spk.at[kind, 0], spk.at[kind, 1]
        from_west, from_east = sst.at[kind, 0], sst.at[kind, 1]
        pairs = (
            (wide.at[:, pl.ds(HALO, HALO), :], wide.at[:, pl.ds(HALO + ROWS, HALO), :]),
            (wide.at[:, pl.ds(ROWS, HALO), :], wide.at[:, pl.ds(0, HALO), :]),
            (west, from_east.at[pl.ds(HALO, ROWS), :]),
            (east, from_west.at[pl.ds(HALO, ROWS), :]),
            (west.at[pl.ds(0, HALO), :], from_east.at[pl.ds(HALO + ROWS, HALO), :]),
            (east.at[pl.ds(0, HALO), :], from_west.at[pl.ds(HALO + ROWS, HALO), :]),
            (west.at[pl.ds(ROWS - HALO, HALO), :], from_east.at[pl.ds(0, HALO), :]),
            (east.at[pl.ds(ROWS - HALO, HALO), :], from_west.at[pl.ds(0, HALO), :]),
        )
        return [
            remote(src, dst, ssend.at[kind, way], srecv.at[kind, way], there(*WAYS[way]))
            for way, (src, dst) in enumerate(pairs)
        ]

    def share_state(kind):
        for k in range(8):
            at = HALO + 8 * k
            a = sext[kind, 0, at : at + 8, :]
            b = sext[kind, 1, at : at + 8, :]
            spk[kind, 0, 8 * k : 8 * k + 8, :] = jnp.where(lane < 8, a, pltpu.roll(b, 8, 1))
            spk[kind, 1, 8 * k : 8 * k + 8, :] = jnp.where(lane < 8, pltpu.roll(a, 8, 1), pltpu.roll(b, 16, 1))
        msgs = state_messages(kind)
        for msg in msgs:
            msg.start()
        return msgs

    keep_north = jnp.where((gy == 0) & (block == 0), 0.0, 1.0)
    keep_south = jnp.where((gy == n_gy - 1) & (block == 7), 0.0, 1.0)
    keep_west = jnp.where((gx == 0) & (sub == 0), 0.0, 1.0)
    keep_east = jnp.where((gx == n_gx - 1) & (sub == 7), 0.0, 1.0)
    masks = (keep_north, keep_south, keep_west, keep_east)
    near_west = jnp.where((gx == 0) & (sub == 7), 0.0, 1.0)
    near_east = jnp.where((gx == n_gx - 1) & (sub == 0), 0.0, 1.0)

    def turn_state(kind):
        west = by_rows(sst, kind, 0)
        east = by_rows(sst, kind, 1)
        levels = [by_rows(sext, kind, lev) for lev in range(LEVELS)]

        def keep(r, value):
            if r == 7:
                value = value * keep_north
            if r == 2:
                value = value * keep_south
            return value

        for r in range(NR):
            across = jnp.concatenate([levels[0][r], levels[1][r]] * 8, axis=0).T
            for k in range(16):
                gt[r, HALO + 8 * k : HALO + 8 * k + 8, :] = keep(r, across[8 * k : 8 * k + 8])
        for base in (0, 8):
            steps = range(base, min(base + 8, NR))
            both = []
            for lev in range(LEVELS):
                out = jnp.zeros((8, 128), F32)
                for r in steps:
                    at = 16 * (r - base)
                    w = west[r] if at == 8 * lev else pltpu.roll(west[r], (128 + at - 8 * lev) % 128, 1)
                    e = east[r] if at + 8 == 8 * lev else pltpu.roll(east[r], (128 + at + 8 - 8 * lev) % 128, 1)
                    out = jnp.where((lane >= at) & (lane < at + 8), w, out)
                    out = jnp.where((lane >= at + 8) & (lane < at + 16), e, out)
                both.append(out)
            across = jnp.concatenate(both * 8, axis=0).T
            for r in steps:
                at = 16 * (r - base)
                gt[r, 0:8, :] = keep(r, across[at : at + 8] * near_west)
                gt[r, HALO + COLS : ECOLS, :] = keep(r, across[at + 8 : at + 16] * near_east)

    def turn_ensemble(c):
        def one(r, carry):
            across = jnp.concatenate([ext[c * PER + q, pl.ds(r, 8, stride=NR), :] for q in range(PER)], axis=0).T
            xt[c, r, HALO : HALO + COLS, :] = across
            return carry

        lax.fori_loop(0, NR, one, 0)

    def column(ref, t, *lead):
        return ref[(*lead, pl.ds(t, 8, stride=NT), slice(None))]

    def put_column(ref, t, value, *lead):
        ref[(*lead, pl.ds(t, 8, stride=NT), slice(None))] = value

    def apply(kind, c):
        def from_work(i):
            return lambda r, t: work[i, r, 8 * t : 8 * t + 8, :]

        def to_work(i):
            def store(r, t, value):
                work[i, r, 8 * t : 8 * t + 8, :] = value

            return store

        norms = {}

        def to_field(r, t, value):
            put_column(ft, t, value, kind, c, r)
            key = 3 * ((t >= 8) + (t >= 10)) + (r >= 2) + (r >= 8)
            norms[key] = norms[key] + value * value if key in norms else value * value

        def to_image(r, t, value):
            put_column(acc, t, column(acc, t, r) + value * column(xt, t, c, r), r)

        sweep(lambda r, t: column(xt, t, c, r) * column(gt, t, r), to_work(0), masks)
        sweep(from_work(0), to_work(1), masks)
        sweep(from_work(1), to_work(0), masks)
        sweep(from_work(0), to_field, masks)
        for key, value in norms.items():
            squares[kind, key] += value
        sweep(lambda r, t: column(ft, t, kind, c, r), to_work(1), masks)
        sweep(from_work(1), to_work(0), masks)
        sweep(from_work(0), to_work(1), masks)
        sweep(from_work(1), to_image, masks)

    group = lane >> 4

    def state_image(kind):
        def over_members(v):
            v = v + pltpu.roll(v, 16, 1)
            v = v + pltpu.roll(v, 32, 1)
            return v + pltpu.roll(v, 64, 1)

        most, last = [], []
        for k in range(16):
            a = [acc[r, HALO + 8 * k : HALO + 8 * k + 8, :] for r in range(NR)]
            s = a[:8]
            for bit in (1, 2, 4):
                odd = (group & bit) != 0
                s = [jnp.where(odd, s[(i + bit) % 8], s[i]) for i in range(8)]
            s = [s[i] + pltpu.roll(s[i + 1], 16, 1) for i in (0, 2, 4, 6)]
            s = [s[i] + pltpu.roll(s[i + 1], 32, 1) for i in (0, 2)]
            most.append(s[0] + pltpu.roll(s[1], 64, 1))
            last.append(jnp.where(lane < 16, over_members(a[8]), over_members(a[9])))
        most = jnp.concatenate(most, axis=0).T
        last = jnp.concatenate(last, axis=0).T
        for r in range(NR):
            for lev in range(LEVELS):
                at = 16 * (r % 8) + 8 * lev
                value = most[at : at + 8] if r < 8 else last[at : at + 8]
                image[kind, lev, 8 * r : 8 * r + 8, :] = value * FILTER_SCALE

    squares[...] = jnp.zeros_like(squares)
    acc[...] = jnp.zeros_like(acc)
    smsgs = share_state(0)

    def ready(c):
        for msg in row_messages(c):
            msg.wait_recv()
        turn_ensemble(c)
        for msg in column_messages(c):
            msg.start()

    ready(0)
    for msg in smsgs:
        msg.wait_recv()
    turn_state(0)

    def first_pass(c, carry):
        @pl.when(c < CHUNKS)
        def _():
            ready(c)

        for msg in column_messages(c - 1):
            msg.wait_recv()
        apply(0, c - 1)
        return carry

    lax.fori_loop(1, CHUNKS + 1, first_pass, 0)
    state_image(0)

    for lev in range(LEVELS):
        v = [a * b for a, b in zip(tiles(image, 0, lev), by_rows(dext, lev))]
        put_rows(sinc, [a * FILTER_SCALE for a in v], lev)
        sext[1, lev, HALO : HALO + ROWS, :] = sinc[lev, HALO : HALO + ROWS, :]
    vmsgs = share_state(1)
    acc[...] = jnp.zeros_like(acc)
    for msg in vmsgs:
        msg.wait_recv()
    turn_state(1)

    def second_pass(c, carry):
        apply(1, c)
        return carry

    lax.fori_loop(0, CHUNKS, second_pass, 0)
    state_image(1)

    def norm(kind):
        parts = []
        for key in range(9):
            inside = None
            for test in (
                [sub > 0] if key // 3 == 0 else [sub < 7] if key // 3 == 2 else []
            ) + ([block > 0] if key % 3 < 2 else []) + ([block < 7] if key % 3 > 0 else []):
                inside = test if inside is None else inside & test
            parts.append(jnp.where(inside, squares[kind, key], 0.0))
        return jnp.sum(total(parts))

    def weighted(kind):
        parts = []
        for lev in range(LEVELS):
            parts += [b * (a * a) for a, b in zip(tiles(image, kind, lev), by_rows(dext, lev))]
        return jnp.sum(total(parts))

    mine = (norm(0), weighted(0), norm(1), weighted(1))
    line = lane[0:1]
    row = jnp.where(line < 64, jnp.where(line < 32, mine[0], mine[1]), jnp.where(line < 96, mine[2], mine[3]))

    def gather(value, ref, me, n, send, recv, to):
        ref[me] = value
        copies = [remote(ref.at[me], ref.at[me], send.at[k], recv.at[k], to(k)) for k in range(1, n)]
        for copy in copies:
            copy.start()
        for copy in copies:
            copy.wait_recv()
        return copies, jnp.sum(ref[...], axis=0)

    acopies, row = gather(row, rowa, gx, n_gx, asend, arecv, lambda k: there(0, k))
    bcopies, row = gather(row, rowb, gy, n_gy, bsend, brecv, lambda k: there(k, 0))

    sums = [jnp.full((8, 128), jnp.sum(jnp.where(line == 32 * i, row, 0.0)), F32) for i in range(4)]
    bnorm_sq = sums[0] + EPS
    bnorm = jnp.sqrt(bnorm_sq)
    unit, cross, square, cube = [s / bnorm_sq for s in sums]
    alpha_one = unit + cross
    shift = 1.0 - alpha_one
    remain_sq = jnp.maximum(shift * shift * unit + 2.0 * shift * cross + square, 0.0)
    beta_sq = remain_sq + EPS
    beta = jnp.sqrt(beta_sq)
    curve = jnp.maximum(shift * shift * cross + 2.0 * shift * square + cube, 0.0)
    alpha_two = (remain_sq + curve) / beta_sq
    determ = alpha_one * alpha_two - beta_sq
    coef_one = bnorm * alpha_two / determ
    coef_two = -bnorm * beta / determ
    on_base = coef_one / bnorm + coef_two * shift / (bnorm * beta)
    on_grown = coef_two / (bnorm * beta)

    outs = []
    for lev in range(LEVELS):
        x, z = tiles(image, 0, lev), tiles(image, 1, lev)
        put_rows(sinc, [on_base * a + on_grown * b for a, b in zip(x, z)], lev)
    outs.append(pltpu.make_async_copy(sinc.at[:, pl.ds(HALO, ROWS), :], increment, out_sem.at[0]))
    outs[-1].start()

    for c in range(CHUNKS):

        def finish(r, carry):
            mixed = []
            for k in range(16):
                at = slice(HALO + 8 * k, HALO + 8 * k + 8)
                mixed.append(on_base * ft[0, c, r, at, :] + on_grown * ft[1, c, r, at, :])
            mixed = jnp.concatenate(mixed, axis=0).T
            for q in range(PER):
                staged[c * PER + q, pl.ds(r, 8, stride=NR), :] = mixed[8 * q : 8 * q + 8]
            return carry

        lax.fori_loop(0, NR, finish, 0)
        outs.append(
            pltpu.make_async_copy(
                staged.at[pl.ds(c * PER, PER), pl.ds(HALO, ROWS), :], control.at[pl.ds(c * PER, PER)], out_sem.at[1 + c]
            )
        )
        outs[-1].start()
    for out in outs:
        out.wait()
    for c in range(CHUNKS):
        for msg in row_messages(c) + column_messages(c):
            msg.wait_send()
    for msg in smsgs + vmsgs + acopies + bcopies:
        msg.wait_send()


def solution(mesh):
    n_gy, n_gx = mesh.shape["gy"], mesh.shape["gx"]

    def on_device(ensemble, obs_cell, obs_level, innovation, obs_weight):
        obs = obs_cell.shape[-1]
        fields = MEMBERS * LEVELS
        vmem = pltpu.VMEM
        dma = pltpu.SemaphoreType.DMA
        control, increment = pl.pallas_call(
            lambda *refs: kernel(n_gy, n_gx, *refs),
            name="lanczos",
            out_shape=(
                jax.ShapeDtypeStruct((fields, ROWS, COLS), F32),
                jax.ShapeDtypeStruct((LEVELS, ROWS, COLS), F32),
            ),
            in_specs=[pl.BlockSpec(memory_space=pl.ANY)] * 5,
            out_specs=(pl.BlockSpec(memory_space=pl.ANY),) * 2,
            scratch_shapes=[
                vmem((fields, ROWS, COLS), BF16),
                vmem((1, 1, obs), jnp.int32),
                vmem((1, 1, obs), jnp.int32),
                vmem((1, 1, obs), F32),
                vmem((1, 1, obs), F32),
                vmem((fields, EROWS, COLS), F32),
                vmem((CHUNKS, NR, ECOLS, 128), F32),
                vmem((NR, ECOLS, 128), F32),
                vmem((2, LEVELS, EROWS, COLS), F32),
                vmem((2, 2, ROWS, COLS), F32),
                vmem((2, 2, EROWS, COLS), F32),
                vmem((LEVELS, EROWS, COLS), F32),
                vmem((6 * ROWS, LEVELS * COLS), F32),
                vmem((2, NR, ECOLS, 128), F32),
                vmem((2, CHUNKS, NR, ECOLS, 128), F32),
                vmem((NR, ECOLS, 128), F32),
                vmem((2, 9, 8, 128), F32),
                vmem((2, LEVELS, EROWS, COLS), F32),
                vmem((n_gx, 1, COLS), F32),
                vmem((n_gy, 1, COLS), F32),
                vmem((fields, EROWS, COLS), F32),
                vmem((LEVELS, EROWS, COLS), F32),
                dma((5,)),
                dma((CHUNKS, 4)),
                dma((CHUNKS, 4)),
                dma((2, 8)),
                dma((2, 8)),
                dma((n_gx,)),
                dma((n_gx,)),
                dma((n_gy,)),
                dma((n_gy,)),
                dma((1 + CHUNKS,)),
            ],
            compiler_params=pltpu.CompilerParams(
                collective_id=0, has_side_effects=True, vmem_limit_bytes=60 * 1024 * 1024
            ),
        )(ensemble.reshape(fields, ROWS, COLS), obs_cell, obs_level, innovation, obs_weight)
        return control.reshape(MEMBERS, LEVELS, ROWS, COLS), increment

    return jax.shard_map(
        on_device,
        mesh=mesh,
        in_specs=(P(None, None, "gy", "gx"),) + (P("gy", "gx", None),) * 4,
        out_specs=(P(None, None, "gy", "gx"), P(None, "gy", "gx")),
        check_vma=False,
    )
```

profile of v0, /device:TPU:0, one launch (start us, length us, event | category | flops | bytes accessed | tf_op | source)
XLA Modules:
  0.0 55.1 jit_solution(1292077481561289969)
XLA Ops:
  0.6 50.6 %lanczos.1 = (f32[64,64,128]{2,1,0:T(8,128)}, f32[2,64,128]{2,1,0:T(8,128)}) custom-call(bf16[64,64,128]{2,1,0:T(8,128)(2,1)} %bitcast.3, s32[1,1,2048]{2,1,0:T(1,128)} %refs_1_.1, s32[1,1,2048]{2,1,0:T(1,128)} %refs_2_.1, f32[1,1,2048]{2,1,0:T(1,128)} %refs_3_.1, f32[1,1,2048]{2,1,0:T(1,128)} %refs_4_.1), custom_call_target="tpu_custom_call" | custom-call | tf_op jit(solution)/shard_map/lanczos/pallas_call | solution.py:511
  51.3 0.0 copy-start
  51.3 3.2 %copy.9 = f32[32,2,64,128]{3,2,1,0:T(8,128)} copy(f32[32,2,64,128]{3,2,1,0:T(8,128)} %bitcast.2) | data formatting | bytes 4194304
  54.5 0.0 copy-done
  54.5 0.6 %copy.10 = f32[2,64,128]{2,1,0:T(8,128)} copy(f32[2,64,128]{2,1,0:T(8,128)S(1)} %copy-done) | data formatting | bytes 131072
Async XLA Ops:
  51.3 3.2 %copy-start = (f32[2,64,128]{2,1,0:T(8,128)S(1)}, f32[2,64,128]{2,1,0:T(8,128)}, u32[]{:S(2)}) copy-start(f32[2,64,128]{2,1,0:T(8,128)} %get-tuple-element.9) | copy-start | bytes 196612
where the time goes:
time: 55.3 us; the launch traced here: 55.1 us
  Pallas kernels  50.6 us (92%)
  local copies, waits for them, and re-layouts  3.82 us (7%)
  between operations  0.65 us (1%)
    pallas_call x1, Pallas kernels, on_device(): pl.pallas_call(lambda *refs: kernel(n_gy, n_gx, *refs), name='lanczos', o...  50.6 us
    unnamed x4, local copies, waits for them, and re-layouts  3.82 us

commit v1 on v0

--- a/solution.py
+++ b/solution.py
@@ -22,6 +22,8 @@
 CHUNKS = 4
 PER = 16
 OBS_STEP = 512
+BATCHES = 8
+BATCH = MEMBERS * LEVELS // BATCHES
 
 WAYS = ((-1, 0), (1, 0), (0, -1), (0, 1), (-1, -1), (-1, 1), (1, -1), (1, 1))
 
@@ -49,6 +51,15 @@
 def put_tiles(ref, values, *lead):
     for r in range(NR):
         ref[(*lead, slice(8 * r, 8 * r + 8), slice(None))] = values[r]
+
+
+def halves(x):
+    high = x.astype(BF16)
+    return jnp.concatenate([high, (x - high.astype(F32)).astype(BF16)], axis=1)
+
+
+def turned(left, right):
+    return lax.dot_general(left, right, (((1,), (1,)), ((), ())), preferred_element_type=F32)
 
 
 def sweep(load, store, masks):
@@ -103,8 +114,10 @@
     level,
     innov,
     weight,
-    control,
-    increment,
+    base_out,
+    grown_out,
+    image,
+    coef,
     xin,
     cin,
     lin,
@@ -122,11 +135,8 @@
     ft,
     acc,
     squares,
-    image,
     rowa,
     rowb,
-    staged,
-    sinc,
     in_sem,
     xsend,
     xrecv,
@@ -136,13 +146,18 @@
     arecv,
     bsend,
     brecv,
-    out_sem,
 ):
     gy = lax.axis_index("gy")
     gx = lax.axis_index("gx")
     lane = lax.broadcasted_iota(jnp.int32, (8, 128), 1)
     sub = lax.broadcasted_iota(jnp.int32, (8, 128), 0)
     block = lane & 7
+    down = lax.broadcasted_iota(jnp.int32, (128, 128), 0)
+    across = lax.broadcasted_iota(jnp.int32, (128, 128), 1)
+    unit_one = jnp.where(down == across, 1.0, 0.0).astype(BF16)
+    unit_two = jnp.concatenate([unit_one, unit_one], axis=1)
+    members = jnp.where(down[:16] == (across[:16] & 15), 1.0, 0.0).astype(BF16)
+    members = jnp.concatenate([members, members], axis=1)
 
     loads = [
         pltpu.make_async_copy(src, dst, in_sem.at[i])
@@ -275,35 +290,35 @@
                 value = value * keep_south
             return value
 
+        right = []
         for r in range(NR):
-            across = jnp.concatenate([levels[0][r], levels[1][r]] * 8, axis=0).T
-            for k in range(16):
-                gt[r, HALO + 8 * k : HALO + 8 * k + 8, :] = keep(r, across[8 * k : 8 * k + 8])
+            right += [halves(jnp.concatenate([levels[0][r], levels[1][r]], axis=0))] * 8
         for base in (0, 8):
-            steps = range(base, min(base + 8, NR))
             both = []
             for lev in range(LEVELS):
                 out = jnp.zeros((8, 128), F32)
-                for r in steps:
+                for r in range(base, min(base + 8, NR)):
                     at = 16 * (r - base)
                     w = west[r] if at == 8 * lev else pltpu.roll(west[r], (128 + at - 8 * lev) % 128, 1)
                     e = east[r] if at + 8 == 8 * lev else pltpu.roll(east[r], (128 + at + 8 - 8 * lev) % 128, 1)
                     out = jnp.where((lane >= at) & (lane < at + 8), w, out)
                     out = jnp.where((lane >= at + 8) & (lane < at + 16), e, out)
                 both.append(out)
-            across = jnp.concatenate(both * 8, axis=0).T
-            for r in steps:
-                at = 16 * (r - base)
-                gt[r, 0:8, :] = keep(r, across[at : at + 8] * near_west)
-                gt[r, HALO + COLS : ECOLS, :] = keep(r, across[at + 8 : at + 16] * near_east)
+            right += [halves(jnp.concatenate(both, axis=0))] * 8
+        out = turned(unit_two, jnp.concatenate(right, axis=0))
+        for r in range(NR):
+            for k in range(16):
+                gt[r, HALO + 8 * k : HALO + 8 * k + 8, :] = keep(r, out[8 * k : 8 * k + 8, 128 * r : 128 * r + 128])
+            at = 16 * (r % 8)
+            side = slice(128 * (NR + r // 8), 128 * (NR + r // 8) + 128)
+            gt[r, 0:8, :] = keep(r, out[at : at + 8, side] * near_west)
+            gt[r, HALO + COLS : ECOLS, :] = keep(r, out[at + 8 : at + 16, side] * near_east)
 
     def turn_ensemble(c):
-        def one(r, carry):
-            across = jnp.concatenate([ext[c * PER + q, pl.ds(r, 8, stride=NR), :] for q in range(PER)], axis=0).T
-            xt[c, r, HALO : HALO + COLS, :] = across
-            return carry
-
-        lax.fori_loop(0, NR, one, 0)
+        right = [ext[c * PER + q, pl.ds(r, 8, stride=NR), :] for r in range(NR) for q in range(PER)]
+        out = turned(unit_one, jnp.concatenate(right, axis=0).astype(BF16))
+        for r in range(NR):
+            xt[c, r, HALO : HALO + COLS, :] = out[:, 128 * r : 128 * r + 128]
 
     def column(ref, t, *lead):
         return ref[(*lead, pl.ds(t, 8, stride=NT), slice(None))]
@@ -342,32 +357,22 @@
         sweep(from_work(0), to_work(1), masks)
         sweep(from_work(1), to_image, masks)
 
-    group = lane >> 4
-
     def state_image(kind):
-        def over_members(v):
-            v = v + pltpu.roll(v, 16, 1)
-            v = v + pltpu.roll(v, 32, 1)
-            return v + pltpu.roll(v, 64, 1)
-
-        most, last = [], []
-        for k in range(16):
-            a = [acc[r, HALO + 8 * k : HALO + 8 * k + 8, :] for r in range(NR)]
-            s = a[:8]
-            for bit in (1, 2, 4):
-                odd = (group & bit) != 0
-                s = [jnp.where(odd, s[(i + bit) % 8], s[i]) for i in range(8)]
-            s = [s[i] + pltpu.roll(s[i + 1], 16, 1) for i in (0, 2, 4, 6)]
-            s = [s[i] + pltpu.roll(s[i + 1], 32, 1) for i in (0, 2)]
-            most.append(s[0] + pltpu.roll(s[1], 64, 1))
-            last.append(jnp.where(lane < 16, over_members(a[8]), over_members(a[9])))
-        most = jnp.concatenate(most, axis=0).T
-        last = jnp.concatenate(last, axis=0).T
         for r in range(NR):
+            out = turned(members, halves(acc[r, HALO : HALO + COLS, :])) * FILTER_SCALE
             for lev in range(LEVELS):
-                at = 16 * (r % 8) + 8 * lev
-                value = most[at : at + 8] if r < 8 else last[at : at + 8]
-                image[kind, lev, 8 * r : 8 * r + 8, :] = value * FILTER_SCALE
+                image[kind, lev, pl.ds(r, 8, stride=NR), :] = out[8 * lev : 8 * lev + 8]
+
+    def turn_back(kind, out_ref, chunks):
+        def one(i, carry):
+            c = i // NR
+            r = lax.rem(i, NR)
+            out = turned(unit_two, halves(ft[kind, c, r, HALO : HALO + COLS, :]))
+            for q in range(PER):
+                out_ref[c * PER + q, pl.ds(r, 8, stride=NR), :] = out[8 * q : 8 * q + 8]
+            return carry
+
+        lax.fori_loop(chunks[0] * NR, chunks[1] * NR, one, 0, unroll=2)
 
     squares[...] = jnp.zeros_like(squares)
     acc[...] = jnp.zeros_like(acc)
@@ -399,11 +404,11 @@
     state_image(0)
 
     for lev in range(LEVELS):
-        v = [a * b for a, b in zip(tiles(image, 0, lev), by_rows(dext, lev))]
-        put_rows(sinc, [a * FILTER_SCALE for a in v], lev)
-        sext[1, lev, HALO : HALO + ROWS, :] = sinc[lev, HALO : HALO + ROWS, :]
+        inner = slice(HALO, HALO + ROWS)
+        sext[1, lev, inner, :] = image[0, lev, inner, :] * dext[lev, inner, :] * FILTER_SCALE
     vmsgs = share_state(1)
     acc[...] = jnp.zeros_like(acc)
+    turn_back(0, base_out, (0, CHUNKS))
     for msg in vmsgs:
         msg.wait_recv()
     turn_state(1)
@@ -429,24 +434,27 @@
     def weighted(kind):
         parts = []
         for lev in range(LEVELS):
-            parts += [b * (a * a) for a, b in zip(tiles(image, kind, lev), by_rows(dext, lev))]
+            for k in range(ROWS // 8):
+                at = slice(HALO + 8 * k, HALO + 8 * k + 8)
+                parts.append(dext[lev, at, :] * (image[kind, lev, at, :] * image[kind, lev, at, :]))
         return jnp.sum(total(parts))
 
     mine = (norm(0), weighted(0), norm(1), weighted(1))
     line = lane[0:1]
     row = jnp.where(line < 64, jnp.where(line < 32, mine[0], mine[1]), jnp.where(line < 96, mine[2], mine[3]))
 
-    def gather(value, ref, me, n, send, recv, to):
+    def gather(value, ref, me, n, send, recv, to, chunks):
         ref[me] = value
         copies = [remote(ref.at[me], ref.at[me], send.at[k], recv.at[k], to(k)) for k in range(1, n)]
         for copy in copies:
             copy.start()
+        turn_back(1, grown_out, chunks)
         for copy in copies:
             copy.wait_recv()
         return copies, jnp.sum(ref[...], axis=0)
 
-    acopies, row = gather(row, rowa, gx, n_gx, asend, arecv, lambda k: there(0, k))
-    bcopies, row = gather(row, rowb, gy, n_gy, bsend, brecv, lambda k: there(k, 0))
+    acopies, row = gather(row, rowa, gx, n_gx, asend, arecv, lambda k: there(0, k), (0, 2))
+    bcopies, row = gather(row, rowb, gy, n_gy, bsend, brecv, lambda k: there(k, 0), (2, CHUNKS))
 
     sums = [jnp.full((8, 128), jnp.sum(jnp.where(line == 32 * i, row, 0.0)), F32) for i in range(4)]
     bnorm_sq = sums[0] + EPS
@@ -465,34 +473,8 @@
     on_base = coef_one / bnorm + coef_two * shift / (bnorm * beta)
     on_grown = coef_two / (bnorm * beta)
 
-    outs = []
-    for lev in range(LEVELS):
-        x, z = tiles(image, 0, lev), tiles(image, 1, lev)
-        put_rows(sinc, [on_base * a + on_grown * b for a, b in zip(x, z)], lev)
-    outs.append(pltpu.make_async_copy(sinc.at[:, pl.ds(HALO, ROWS), :], increment, out_sem.at[0]))
-    outs[-1].start()
-
-    for c in range(CHUNKS):
-
-        def finish(r, carry):
-            mixed = []
-            for k in range(16):
-                at = slice(HALO + 8 * k, HALO + 8 * k + 8)
-                mixed.append(on_base * ft[0, c, r, at, :] + on_grown * ft[1, c, r, at, :])
-            mixed = jnp.concatenate(mixed, axis=0).T
-            for q in range(PER):
-                staged[c * PER + q, pl.ds(r, 8, stride=NR), :] = mixed[8 * q : 8 * q + 8]
-            return carry
-
-        lax.fori_loop(0, NR, finish, 0)
-        outs.append(
-            pltpu.make_async_copy(
-                staged.at[pl.ds(c * PER, PER), pl.ds(HALO, ROWS), :], control.at[pl.ds(c * PER, PER)], out_sem.at[1 + c]
-            )
-        )
-        outs[-1].start()
-    for out in outs:
-        out.wait()
+    coef[0] = on_base
+    coef[1] = on_grown
     for c in range(CHUNKS):
         for msg in row_messages(c) + column_messages(c):
             msg.wait_send()
@@ -500,6 +482,32 @@
         msg.wait_send()
 
 
+def combine(base, grown, image, coef, control, increment, staged, small, out_sem):
+    a, b = coef[0], coef[1]
+    copies = []
+    for i in range(BATCHES):
+
+        def one(k, carry):
+            f = i * BATCH + k
+            for r in range(ROWS // 8):
+                at = slice(HALO + 8 * r, HALO + 8 * r + 8)
+                staged[f, 8 * r : 8 * r + 8, :] = a * base[f, at, :] + b * grown[f, at, :]
+            return carry
+
+        lax.fori_loop(0, BATCH, one, 0, unroll=2)
+        part = pl.ds(i * BATCH, BATCH)
+        copies.append(pltpu.make_async_copy(staged.at[part], control.at[part], out_sem.at[i]))
+        copies[-1].start()
+    for lev in range(LEVELS):
+        for r in range(ROWS // 8):
+            at = slice(HALO + 8 * r, HALO + 8 * r + 8)
+            small[lev, 8 * r : 8 * r + 8, :] = a * image[0, lev, at, :] + b * image[1, lev, at, :]
+    copies.append(pltpu.make_async_copy(small, increment, out_sem.at[BATCHES]))
+    copies[-1].start()
+    for copy in copies:
+        copy.wait()
+
+
 def solution(mesh):
     n_gy, n_gx = mesh.shape["gy"], mesh.shape["gx"]
 
@@ -508,15 +516,17 @@
         fields = MEMBERS * LEVELS
         vmem = pltpu.VMEM
         dma = pltpu.SemaphoreType.DMA
-        control, increment = pl.pallas_call(
+        base, grown, image, coef = pl.pallas_call(
             lambda *refs: kernel(n_gy, n_gx, *refs),
             name="lanczos",
             out_shape=(
-                jax.ShapeDtypeStruct((fields, ROWS, COLS), F32),
-                jax.ShapeDtypeStruct((LEVELS, ROWS, COLS), F32),
+                jax.ShapeDtypeStruct((fields, EROWS, COLS), F32),
+                jax.ShapeDtypeStruct((fields, EROWS, COLS), F32),
+                jax.ShapeDtypeStruct((2, LEVELS, EROWS, COLS), F32),
+                jax.ShapeDtypeStruct((2, 8, COLS), F32),
             ),
-            in_specs=[pl.BlockSpec(memory_space=pl.ANY)] * 5,
-            out_specs=(pl.BlockSpec(memory_space=pl.ANY),) * 2,
+            in_specs=[pl.BlockSpec(memory_space=pltpu.HBM)] * 5,
+            out_specs=(pl.BlockSpec(memory_space=vmem),) * 4,
             scratch_shapes=[
                 vmem((fields, ROWS, COLS), BF16),
                 vmem((1, 1, obs), jnp.int32),
@@ -535,11 +545,8 @@
                 vmem((2, CHUNKS, NR, ECOLS, 128), F32),
                 vmem((NR, ECOLS, 128), F32),
                 vmem((2, 9, 8, 128), F32),
-                vmem((2, LEVELS, EROWS, COLS), F32),
                 vmem((n_gx, 1, COLS), F32),
                 vmem((n_gy, 1, COLS), F32),
-                vmem((fields, EROWS, COLS), F32),
-                vmem((LEVELS, EROWS, COLS), F32),
                 dma((5,)),
                 dma((CHUNKS, 4)),
                 dma((CHUNKS, 4)),
@@ -549,12 +556,32 @@
                 dma((n_gx,)),
                 dma((n_gy,)),
                 dma((n_gy,)),
-                dma((1 + CHUNKS,)),
             ],
             compiler_params=pltpu.CompilerParams(
-                collective_id=0, has_side_effects=True, vmem_limit_bytes=60 * 1024 * 1024
+                collective_id=0, has_side_effects=True, vmem_limit_bytes=28 * 1024 * 1024
             ),
-        )(ensemble.reshape(fields, ROWS, COLS), obs_cell, obs_level, innovation, obs_weight)
+        )(
+            *[
+                pltpu.with_memory_space_constraint(x, pltpu.HBM)
+                for x in (ensemble.reshape(fields, ROWS, COLS), obs_cell, obs_level, innovation, obs_weight)
+            ]
+        )
+        control, increment = pl.pallas_call(
+            combine,
+            name="combine",
+            out_shape=(
+                jax.ShapeDtypeStruct((fields, ROWS, COLS), F32),
+                jax.ShapeDtypeStruct((LEVELS, ROWS, COLS), F32),
+            ),
+            in_specs=[pl.BlockSpec(memory_space=vmem)] * 4,
+            out_specs=(pl.BlockSpec(memory_space=pltpu.HBM),) * 2,
+            scratch_shapes=[
+                vmem((fields, ROWS, COLS), F32),
+                vmem((LEVELS, ROWS, COLS), F32),
+                dma((BATCHES + 1,)),
+            ],
+            compiler_params=pltpu.CompilerParams(vmem_limit_bytes=12 * 1024 * 1024),
+        )(base, grown, image, coef)
         return control.reshape(MEMBERS, LEVELS, ROWS, COLS), increment
 
     return jax.shard_map(

time: 55.3 us -> 46.9 us (0.85)
  Pallas kernels: 50.6 us -> 46.2 us
  local copies, waits for them, and re-layouts: 3.82 us -> 0 us
    pallas_call x1, Pallas kernels: 50.6 us -> 44.7 us  [on_device(): pl.pallas_call(lambda *refs: kernel(n_gy, n_gx, *refs), name='lanczos', o...]
    unnamed x4 -> x0, local copies, waits for them, and re-layouts: 3.82 us -> none
    pallas_call x0 -> x1, Pallas kernels: none -> 1.44 us  [on_device(): pl.pallas_call(combine, name='combine', out_shape=(jax.ShapeDtypeStruct((...]
where the time goes in v1:
time: 46.9 us; the launch traced here: 46.8 us
  Pallas kernels  46.2 us (99%)
  between operations  0.64 us (1%)
    pallas_call x1, Pallas kernels, on_device(): pl.pallas_call(lambda *refs: kernel(n_gy, n_gx, *refs), name='lanczos', o...  44.7 us
    pallas_call x1, Pallas kernels, on_device(): pl.pallas_call(combine, name='combine', out_shape=(jax.ShapeDtypeStruct((...  1.44 us

profile of v1, /device:TPU:0, one launch (start us, length us, event | category | flops | bytes accessed | tf_op | source)
XLA Modules:
  0.0 46.8 jit_solution(15256887446922800803)
XLA Ops:
  0.6 44.7 %lanczos.1 = (f32[64,80,128]{2,1,0:T(8,128)S(1)}, f32[64,80,128]{2,1,0:T(8,128)S(1)}, f32[2,2,80,128]{3,2,1,0:T(8,128)S(1)}, f32[2,8,128]{2,1,0:T(8,128)S(1)}) custom-call(bf16[64,64,128]{2,1,0:T(8,128)(2,1)} %bitcast.2, s32[1,1,2048]{2,1,0:T(1,128)} %refs_1_.1, s32[1,1,2048]{2,1,0:T(1,128)} %refs_2_.1, f32[1,1,2048]{2,1,0:T(1,128)} %refs_3_.1, ...), custom_call_target="tpu_custom_call" | custom-call | tf_op jit(solution)/shard_map/lanczos/pallas_call | solution.py:519
  45.3 1.4 %combine.1 = (f32[64,64,128]{2,1,0:T(8,128)}, f32[2,64,128]{2,1,0:T(8,128)}) custom-call(f32[64,80,128]{2,1,0:T(8,128)S(1)} %get-tuple-element.8.base, f32[64,80,128]{2,1,0:T(8,128)S(1)} %get-tuple-element.9.grown, f32[2,2,80,128]{3,2,1,0:T(8,128)S(1)} %get-tuple-element.10.image, f32[2,8,128]{2,1,0:T(8,128)S(1)} %get-tuple-element.11.coef), custom_call_target="tpu_custom_call" | custom-call | tf_op jit(solution)/shard_map/combine/pallas_call | solution.py:569

commit v2 on v1

--- a/solution.py
+++ b/solution.py
@@ -161,7 +161,10 @@
 
     loads = [
         pltpu.make_async_copy(src, dst, in_sem.at[i])
-        for i, (src, dst) in enumerate(((ens, xin), (cell, cin), (level, lin), (innov, iin), (weight, win)))
+        for i, (src, dst) in enumerate(
+            [(ens.at[pl.ds(c * PER, PER)], xin.at[pl.ds(c * PER, PER)]) for c in range(CHUNKS)]
+            + [(cell, cin), (level, lin), (innov, iin), (weight, win)]
+        )
     ]
     for load in loads:
         load.start()
@@ -179,14 +182,18 @@
     for dy, dx in met:
         pl.semaphore_signal(barrier, inc=1, device_id=there(dy, dx), device_id_type=MESH)
 
-    loads[0].wait()
-
-    def widen(i, carry):
-        for k in range(4):
-            ext[4 * i + k, HALO : HALO + ROWS, :] = xin[4 * i + k].astype(F32)
-        return carry
-
-    lax.fori_loop(0, MEMBERS * LEVELS // 4, widen, 0)
+    def widen(c):
+        loads[c].wait()
+
+        def one(i, carry):
+            for k in range(4):
+                f = c * PER + 4 * i + k
+                ext[f, HALO : HALO + ROWS, :] = xin[f].astype(F32)
+            return carry
+
+        lax.fori_loop(0, PER // 4, one, 0)
+
+    widen(0)
 
     def row_messages(c):
         fields = ext.at[pl.ds(c * PER, PER)]
@@ -203,11 +210,12 @@
         ]
 
     pl.semaphore_wait(barrier, len(met))
-    for c in range(CHUNKS):
-        for msg in row_messages(c):
-            msg.start()
-
-    for load in loads[1:]:
+    for msg in row_messages(0):
+        msg.start()
+    for c in range(1, CHUNKS):
+        widen(c)
+
+    for load in loads[CHUNKS:]:
         load.wait()
     grid[...] = jnp.zeros_like(grid)
 
@@ -363,7 +371,9 @@
             for lev in range(LEVELS):
                 image[kind, lev, pl.ds(r, 8, stride=NR), :] = out[8 * lev : 8 * lev + 8]
 
-    def turn_back(kind, out_ref, chunks):
+    def turn_back(kind, chunks):
+        out_ref = (base_out, grown_out)[kind]
+
         def one(i, carry):
             c = i // NR
             r = lax.rem(i, NR)
@@ -372,11 +382,14 @@
                 out_ref[c * PER + q, pl.ds(r, 8, stride=NR), :] = out[8 * q : 8 * q + 8]
             return carry
 
-        lax.fori_loop(chunks[0] * NR, chunks[1] * NR, one, 0, unroll=2)
-
+        lax.fori_loop(chunks[0] * NR, chunks[1] * NR, one, 0, unroll=5)
+
+    smsgs = share_state(0)
+    for c in range(1, CHUNKS):
+        for msg in row_messages(c):
+            msg.start()
     squares[...] = jnp.zeros_like(squares)
     acc[...] = jnp.zeros_like(acc)
-    smsgs = share_state(0)
 
     def ready(c):
         for msg in row_messages(c):
@@ -389,18 +402,20 @@
     for msg in smsgs:
         msg.wait_recv()
     turn_state(0)
+    ready(1)
 
     def first_pass(c, carry):
-        @pl.when(c < CHUNKS)
+        for msg in column_messages(c):
+            msg.wait_recv()
+        apply(0, c)
+
+        @pl.when(c + 2 < CHUNKS)
         def _():
-            ready(c)
-
-        for msg in column_messages(c - 1):
-            msg.wait_recv()
-        apply(0, c - 1)
+            ready(c + 2)
+
         return carry
 
-    lax.fori_loop(1, CHUNKS + 1, first_pass, 0)
+    lax.fori_loop(0, CHUNKS, first_pass, 0)
     state_image(0)
 
     for lev in range(LEVELS):
@@ -408,7 +423,7 @@
         sext[1, lev, inner, :] = image[0, lev, inner, :] * dext[lev, inner, :] * FILTER_SCALE
     vmsgs = share_state(1)
     acc[...] = jnp.zeros_like(acc)
-    turn_back(0, base_out, (0, CHUNKS))
+    turn_back(0, (0, 3))
     for msg in vmsgs:
         msg.wait_recv()
     turn_state(1)
@@ -443,18 +458,19 @@
     line = lane[0:1]
     row = jnp.where(line < 64, jnp.where(line < 32, mine[0], mine[1]), jnp.where(line < 96, mine[2], mine[3]))
 
-    def gather(value, ref, me, n, send, recv, to, chunks):
+    def gather(value, ref, me, n, send, recv, to, fill):
         ref[me] = value
         copies = [remote(ref.at[me], ref.at[me], send.at[k], recv.at[k], to(k)) for k in range(1, n)]
         for copy in copies:
             copy.start()
-        turn_back(1, grown_out, chunks)
+        for kind, chunks in fill:
+            turn_back(kind, chunks)
         for copy in copies:
             copy.wait_recv()
         return copies, jnp.sum(ref[...], axis=0)
 
-    acopies, row = gather(row, rowa, gx, n_gx, asend, arecv, lambda k: there(0, k), (0, 2))
-    bcopies, row = gather(row, rowb, gy, n_gy, bsend, brecv, lambda k: there(k, 0), (2, CHUNKS))
+    acopies, row = gather(row, rowa, gx, n_gx, asend, arecv, lambda k: there(0, k), [(0, (3, 4)), (1, (0, 1))])
+    bcopies, row = gather(row, rowb, gy, n_gy, bsend, brecv, lambda k: there(k, 0), [(1, (1, 4))])
 
     sums = [jnp.full((8, 128), jnp.sum(jnp.where(line == 32 * i, row, 0.0)), F32) for i in range(4)]
     bnorm_sq = sums[0] + EPS
@@ -547,7 +563,7 @@
                 vmem((2, 9, 8, 128), F32),
                 vmem((n_gx, 1, COLS), F32),
                 vmem((n_gy, 1, COLS), F32),
-                dma((5,)),
+                dma((CHUNKS + 4,)),
                 dma((CHUNKS, 4)),
                 dma((CHUNKS, 4)),
                 dma((2, 8)),

time: 46.9 us -> 44.1 us (0.940)
  Pallas kernels: 46.2 us -> 43.3 us
    pallas_call x1, Pallas kernels: 44.7 us -> 41.8 us  [on_device(): pl.pallas_call(lambda *refs: kernel(n_gy, n_gx, *refs), name='lanczos', o...]
where the time goes in v2:
time: 44.1 us; the launch traced here: 43.9 us
  Pallas kernels  43.3 us (98%)
  between operations  0.64 us (1%)
    pallas_call x1, Pallas kernels, on_device(): pl.pallas_call(lambda *refs: kernel(n_gy, n_gx, *refs), name='lanczos', o...  41.8 us
    pallas_call x1, Pallas kernels, on_device(): pl.pallas_call(combine, name='combine', out_shape=(jax.ShapeDtypeStruct((...  1.44 us

profile of v2, /device:TPU:0, one launch (start us, length us, event | category | flops | bytes accessed | tf_op | source)
XLA Modules:
  0.0 43.9 jit_solution(4584611908865923476)
XLA Ops:
  0.6 41.8 %lanczos.1 = (f32[64,80,128]{2,1,0:T(8,128)S(1)}, f32[64,80,128]{2,1,0:T(8,128)S(1)}, f32[2,2,80,128]{3,2,1,0:T(8,128)S(1)}, f32[2,8,128]{2,1,0:T(8,128)S(1)}) custom-call(bf16[64,64,128]{2,1,0:T(8,128)(2,1)} %bitcast.2, s32[1,1,2048]{2,1,0:T(1,128)} %refs_1_.1, s32[1,1,2048]{2,1,0:T(1,128)} %refs_2_.1, f32[1,1,2048]{2,1,0:T(1,128)} %refs_3_.1, ...), custom_call_target="tpu_custom_call" | custom-call | tf_op jit(solution)/shard_map/lanczos/pallas_call | solution.py:535
  42.5 1.4 %combine.1 = (f32[64,64,128]{2,1,0:T(8,128)}, f32[2,64,128]{2,1,0:T(8,128)}) custom-call(f32[64,80,128]{2,1,0:T(8,128)S(1)} %get-tuple-element.8.base, f32[64,80,128]{2,1,0:T(8,128)S(1)} %get-tuple-element.9.grown, f32[2,2,80,128]{3,2,1,0:T(8,128)S(1)} %get-tuple-element.10.image, f32[2,8,128]{2,1,0:T(8,128)S(1)} %get-tuple-element.11.coef), custom_call_target="tpu_custom_call" | custom-call | tf_op jit(solution)/shard_map/combine/pallas_call | solution.py:585

commit v3 on v2

--- a/solution.py
+++ b/solution.py
@@ -124,10 +124,16 @@
     iin,
     win,
     ext,
+    rhalo,
+    eside,
+    cpack,
+    corner,
     xt,
     gt,
     sext,
     spk,
+    sthin,
+    sland,
     sst,
     dext,
     grid,
@@ -140,6 +146,8 @@
     in_sem,
     xsend,
     xrecv,
+    csend,
+    crecv,
     ssend,
     srecv,
     asend,
@@ -182,39 +190,6 @@
     for dy, dx in met:
         pl.semaphore_signal(barrier, inc=1, device_id=there(dy, dx), device_id_type=MESH)
 
-    def widen(c):
-        loads[c].wait()
-
-        def one(i, carry):
-            for k in range(4):
-                f = c * PER + 4 * i + k
-                ext[f, HALO : HALO + ROWS, :] = xin[f].astype(F32)
-            return carry
-
-        lax.fori_loop(0, PER // 4, one, 0)
-
-    widen(0)
-
-    def row_messages(c):
-        fields = ext.at[pl.ds(c * PER, PER)]
-        return [
-            remote(fields.at[:, pl.ds(src, HALO), :], fields.at[:, pl.ds(dst, HALO), :], xsend.at[c, way], xrecv.at[c, way], there(*WAYS[way]))
-            for way, (src, dst) in enumerate(((HALO, HALO + ROWS), (ROWS, 0)))
-        ]
-
-    def column_messages(c):
-        fields = xt.at[c]
-        return [
-            remote(fields.at[:, pl.ds(src, HALO), :], fields.at[:, pl.ds(dst, HALO), :], xsend.at[c, way], xrecv.at[c, way], there(*WAYS[way]))
-            for way, (src, dst) in ((2, (HALO, HALO + COLS)), (3, (COLS, 0)))
-        ]
-
-    pl.semaphore_wait(barrier, len(met))
-    for msg in row_messages(0):
-        msg.start()
-    for c in range(1, CHUNKS):
-        widen(c)
-
     for load in loads[CHUNKS:]:
         load.wait()
     grid[...] = jnp.zeros_like(grid)
@@ -230,7 +205,7 @@
         right = jnp.where(on_col, 1.0, 0.0).astype(BF16)
         left = []
         for value in (w * iin[0, :, part], w):
-            for _ in range(3):
+            for _ in range(2):
                 piece = value.astype(BF16).astype(F32)
                 left.append(jnp.where(on_row, piece, 0.0).astype(BF16))
                 value = value - piece
@@ -241,12 +216,90 @@
     lax.fori_loop(0, cin.shape[-1] // OBS_STEP, scatter, 0)
     for lev in range(LEVELS):
         cols = slice(lev * COLS, lev * COLS + COLS)
-        grad = grid[0:64, cols] + (grid[64:128, cols] + grid[128:192, cols])
-        diag = grid[192:256, cols] + (grid[256:320, cols] + grid[320:384, cols])
+        grad = grid[0:64, cols] + grid[64:128, cols]
+        diag = grid[128:192, cols] + grid[192:256, cols]
         sext[0, lev, HALO : HALO + ROWS, :] = grad * FILTER_SCALE
         dext[lev, 0:HALO, :] = jnp.zeros((HALO, COLS), F32)
         dext[lev, HALO : HALO + ROWS, :] = diag
         dext[lev, HALO + ROWS : EROWS, :] = jnp.zeros((HALO, COLS), F32)
+
+    def widen(c):
+        loads[c].wait()
+
+        def one(i, carry):
+            for k in range(4):
+                f = c * PER + 4 * i + k
+                ext[f, 0:HALO, :] = jnp.zeros((HALO, COLS), F32)
+                ext[f, HALO + ROWS : EROWS, :] = jnp.zeros((HALO, COLS), F32)
+                ext[f, HALO : HALO + ROWS, :] = xin[f].astype(F32)
+            return carry
+
+        lax.fori_loop(0, PER // 4, one, 0)
+
+    widen(0)
+
+    def row_messages(c):
+        fields = pl.ds(c * PER, PER)
+        return [
+            remote(ext.at[fields, pl.ds(src, HALO), :], rhalo.at[fields, pl.ds(dst, HALO), :], xsend.at[c, way], xrecv.at[c, way], there(*WAYS[way]))
+            for way, (src, dst) in enumerate(((HALO, HALO), (ROWS, 0)))
+        ]
+
+    def column_messages(c):
+        return [
+            remote(eside.at[side, c], xt.at[c, :, pl.ds(dst, HALO), :], xsend.at[c, 2 + side], xrecv.at[c, 2 + side], there(*WAYS[2 + side]))
+            for side, dst in ((0, HALO + COLS), (1, 0))
+        ]
+
+    def corner_messages():
+        return [
+            remote(cpack.at[side, :, pl.ds(low, HALO), :], corner.at[3 - k], csend.at[k], crecv.at[k], there(*WAYS[4 + k]))
+            for k, (side, low) in enumerate(((0, 0), (1, 0), (0, HALO), (1, HALO)))
+        ]
+
+    def reversed_eights(x):
+        for width in (1, 2, 4):
+            x = jnp.where((lane & width) == 0, pltpu.roll(x, 128 - width, 1), pltpu.roll(x, width, 1))
+        return x
+
+    def pack_corners(c, carry):
+        for low, at in ((0, HALO), (HALO, ROWS)):
+            west = jnp.zeros((8, 128), F32)
+            east = jnp.zeros((8, 128), F32)
+            for q in range(PER):
+                part = ext[c * PER + q, at : at + HALO, :]
+                here = (lane >= 8 * q) & (lane < 8 * q + 8)
+                west = jnp.where(here, pltpu.roll(part, 8 * q, 1) if q else part, west)
+                east = jnp.where(here, pltpu.roll(part, 8 * q + 8, 1) if q < 15 else part, east)
+            cpack[0, c, low : low + HALO, :] = reversed_eights(west)
+            cpack[1, c, low : low + HALO, :] = reversed_eights(east)
+        return carry
+
+    def turn_right(c):
+        right = [ext[c * PER + q, pl.ds(r, 8, stride=NR), :] for r in range(NR) for q in range(PER)]
+        return jnp.concatenate(right, axis=0).astype(BF16)
+
+    ends = jnp.concatenate([unit_one[0:8].astype(F32), unit_one[120:128].astype(F32)], axis=0).astype(BF16)
+
+    def early_columns(c, carry):
+        out = turned(ends, turn_right(c))
+        for r in range(NR):
+            eside[0, c, r] = out[0:8, 128 * r : 128 * r + 128]
+            eside[1, c, r] = out[8:16, 128 * r : 128 * r + 128]
+        for msg in column_messages(c):
+            msg.start()
+        return carry
+
+    def put_corners(c):
+        for side, at in ((0, 0), (1, HALO + COLS)):
+            for r in range(NR):
+                strip = xt[c, r, at : at + HALO, :]
+                for which, row, b in ((side, r, 0), (2 + side, r - 2, 7)):
+                    if 0 <= row < 8:
+                        line = jnp.broadcast_to(corner[which, c, row : row + 1, :], (8, 128))
+                        line = pltpu.roll(line, 0 if b else 121, 1, stride=1, stride_axis=0)
+                        strip = jnp.where(block == b, line, strip)
+                xt[c, r, at : at + HALO, :] = strip
 
     def state_messages(kind):
         wide, west, east = sext.at[kind], spk.at[kind, 0], spk.at[kind, 1]
@@ -254,12 +307,12 @@
         pairs = (
             (wide.at[:, pl.ds(HALO, HALO), :], wide.at[:, pl.ds(HALO + ROWS, HALO), :]),
             (wide.at[:, pl.ds(ROWS, HALO), :], wide.at[:, pl.ds(0, HALO), :]),
-            (west, from_east.at[pl.ds(HALO, ROWS), :]),
-            (east, from_west.at[pl.ds(HALO, ROWS), :]),
+            (sthin.at[kind, 0], sland.at[kind, 1]),
+            (sthin.at[kind, 1], sland.at[kind, 0]),
             (west.at[pl.ds(0, HALO), :], from_east.at[pl.ds(HALO + ROWS, HALO), :]),
             (east.at[pl.ds(0, HALO), :], from_west.at[pl.ds(HALO + ROWS, HALO), :]),
-            (west.at[pl.ds(ROWS - HALO, HALO), :], from_east.at[pl.ds(0, HALO), :]),
-            (east.at[pl.ds(ROWS - HALO, HALO), :], from_west.at[pl.ds(0, HALO), :]),
+            (west.at[pl.ds(HALO, HALO), :], from_east.at[pl.ds(0, HALO), :]),
+            (east.at[pl.ds(HALO, HALO), :], from_west.at[pl.ds(0, HALO), :]),
         )
         return [
             remote(src, dst, ssend.at[kind, way], srecv.at[kind, way], there(*WAYS[way]))
@@ -267,12 +320,21 @@
         ]
 
     def share_state(kind):
+        thin = [jnp.zeros((8, 128), F32)] * 2
         for k in range(8):
             at = HALO + 8 * k
             a = sext[kind, 0, at : at + 8, :]
             b = sext[kind, 1, at : at + 8, :]
-            spk[kind, 0, 8 * k : 8 * k + 8, :] = jnp.where(lane < 8, a, pltpu.roll(b, 8, 1))
-            spk[kind, 1, 8 * k : 8 * k + 8, :] = jnp.where(lane < 8, pltpu.roll(a, 8, 1), pltpu.roll(b, 16, 1))
+            here = (lane >= 16 * k) & (lane < 16 * k + 8)
+            both = (lane >= 16 * k) & (lane < 16 * k + 16)
+            for side in range(2):
+                first = (16 * k + 8 * side) % 128
+                x = jnp.where(here, pltpu.roll(a, first, 1) if first else a, pltpu.roll(b, (first + 8) % 128, 1) if first != 120 else b)
+                thin[side] = jnp.where(both, x, thin[side])
+        for side in range(2):
+            sthin[kind, side] = thin[side]
+            spk[kind, side, 0:8, :] = thin[side]
+            spk[kind, side, 8:16, :] = pltpu.roll(thin[side], 16, 1)
         msgs = state_messages(kind)
         for msg in msgs:
             msg.start()
@@ -287,6 +349,10 @@
     near_east = jnp.where((gx == n_gx - 1) & (sub == 0), 0.0, 1.0)
 
     def turn_state(kind):
+        for side in range(2):
+            thin = sland[kind, side]
+            for k in range(8):
+                sst[kind, side, HALO + 8 * k : 2 * HALO + 8 * k, :] = pltpu.roll(thin, 128 - 16 * k, 1) if k else thin
         west = by_rows(sst, kind, 0)
         east = by_rows(sst, kind, 1)
         levels = [by_rows(sext, kind, lev) for lev in range(LEVELS)]
@@ -323,8 +389,11 @@
             gt[r, HALO + COLS : ECOLS, :] = keep(r, out[at + 8 : at + 16, side] * near_east)
 
     def turn_ensemble(c):
-        right = [ext[c * PER + q, pl.ds(r, 8, stride=NR), :] for r in range(NR) for q in range(PER)]
-        out = turned(unit_one, jnp.concatenate(right, axis=0).astype(BF16))
+        for q in range(PER):
+            f = c * PER + q
+            ext[f, 0:HALO, :] = rhalo[f, 0:HALO, :]
+            ext[f, HALO + ROWS : EROWS, :] = rhalo[f, HALO : 2 * HALO, :]
+        out = turned(unit_one, turn_right(c))
         for r in range(NR):
             xt[c, r, HALO : HALO + COLS, :] = out[:, 128 * r : 128 * r + 128]
 
@@ -384,35 +453,39 @@
 
         lax.fori_loop(chunks[0] * NR, chunks[1] * NR, one, 0, unroll=5)
 
+    pl.semaphore_wait(barrier, len(met))
+    for msg in row_messages(0):
+        msg.start()
     smsgs = share_state(0)
-    for c in range(1, CHUNKS):
+    widen(1)
+    for msg in row_messages(1):
+        msg.start()
+    for c in range(2, CHUNKS):
+        widen(c)
+    lax.fori_loop(0, CHUNKS, pack_corners, 0)
+    for msg in corner_messages():
+        msg.start()
+    lax.fori_loop(0, CHUNKS, early_columns, 0)
+    for c in range(2, CHUNKS):
         for msg in row_messages(c):
             msg.start()
     squares[...] = jnp.zeros_like(squares)
     acc[...] = jnp.zeros_like(acc)
 
-    def ready(c):
+    for msg in smsgs:
+        msg.wait_recv()
+    turn_state(0)
+    for msg in corner_messages():
+        msg.wait_recv()
+
+    def first_pass(c, carry):
+        for msg in column_messages(c):
+            msg.wait_recv()
+        put_corners(c)
         for msg in row_messages(c):
             msg.wait_recv()
         turn_ensemble(c)
-        for msg in column_messages(c):
-            msg.start()
-
-    ready(0)
-    for msg in smsgs:
-        msg.wait_recv()
-    turn_state(0)
-    ready(1)
-
-    def first_pass(c, carry):
-        for msg in column_messages(c):
-            msg.wait_recv()
         apply(0, c)
-
-        @pl.when(c + 2 < CHUNKS)
-        def _():
-            ready(c + 2)
-
         return carry
 
     lax.fori_loop(0, CHUNKS, first_pass, 0)
@@ -494,7 +567,7 @@
     for c in range(CHUNKS):
         for msg in row_messages(c) + column_messages(c):
             msg.wait_send()
-    for msg in smsgs + vmsgs + acopies + bcopies:
+    for msg in corner_messages() + smsgs + vmsgs + acopies + bcopies:
         msg.wait_send()
 
 
@@ -550,13 +623,19 @@
                 vmem((1, 1, obs), F32),
                 vmem((1, 1, obs), F32),
                 vmem((fields, EROWS, COLS), F32),
+                vmem((fields, 2 * HALO, COLS), F32),
+                vmem((2, CHUNKS, NR, HALO, 128), F32),
+                vmem((2, CHUNKS, 2 * HALO, 128), F32),
+                vmem((4, CHUNKS, HALO, 128), F32),
                 vmem((CHUNKS, NR, ECOLS, 128), F32),
                 vmem((NR, ECOLS, 128), F32),
                 vmem((2, LEVELS, EROWS, COLS), F32),
-                vmem((2, 2, ROWS, COLS), F32),
+                vmem((2, 2, 2 * HALO, COLS), F32),
+                vmem((2, 2, HALO, COLS), F32),
+                vmem((2, 2, HALO, COLS), F32),
                 vmem((2, 2, EROWS, COLS), F32),
                 vmem((LEVELS, EROWS, COLS), F32),
-                vmem((6 * ROWS, LEVELS * COLS), F32),
+                vmem((4 * ROWS, LEVELS * COLS), F32),
                 vmem((2, NR, ECOLS, 128), F32),
                 vmem((2, CHUNKS, NR, ECOLS, 128), F32),
                 vmem((NR, ECOLS, 128), F32),
@@ -566,6 +645,8 @@
                 dma((CHUNKS + 4,)),
                 dma((CHUNKS, 4)),
                 dma((CHUNKS, 4)),
+                dma((4,)),
+                dma((4,)),
                 dma((2, 8)),
                 dma((2, 8)),
                 dma((n_gx,)),

time: 44.1 us -> 41.3 us (0.937)
  Pallas kernels: 43.3 us -> 40.5 us
    pallas_call x1, Pallas kernels: 41.8 us -> 39.1 us  [on_device(): pl.pallas_call(lambda *refs: kernel(n_gy, n_gx, *refs), name='lanczos', o...]
where the time goes in v3:
time: 41.3 us; the launch traced here: 41.2 us
  Pallas kernels  40.5 us (98%)
  between operations  0.64 us (2%)
    pallas_call x1, Pallas kernels, on_device(): pl.pallas_call(lambda *refs: kernel(n_gy, n_gx, *refs), name='lanczos', o...  39.1 us
    pallas_call x1, Pallas kernels, on_device(): pl.pallas_call(combine, name='combine', out_shape=(jax.ShapeDtypeStruct((...  1.44 us

profile of v3, /device:TPU:0, one launch (start us, length us, event | category | flops | bytes accessed | tf_op | source)
XLA Modules:
  0.0 41.2 jit_solution(12990531749392745555)
XLA Ops:
  0.6 39.1 %lanczos.1 = (f32[64,80,128]{2,1,0:T(8,128)S(1)}, f32[64,80,128]{2,1,0:T(8,128)S(1)}, f32[2,2,80,128]{3,2,1,0:T(8,128)S(1)}, f32[2,8,128]{2,1,0:T(8,128)S(1)}) custom-call(bf16[64,64,128]{2,1,0:T(8,128)(2,1)} %bitcast.2, s32[1,1,2048]{2,1,0:T(1,128)} %refs_1_.1, s32[1,1,2048]{2,1,0:T(1,128)} %refs_2_.1, f32[1,1,2048]{2,1,0:T(1,128)} %refs_3_.1, ...), custom_call_target="tpu_custom_call" | custom-call | tf_op jit(solution)/shard_map/lanczos/pallas_call | solution.py:608
  39.7 1.4 %combine.1 = (f32[64,64,128]{2,1,0:T(8,128)}, f32[2,64,128]{2,1,0:T(8,128)}) custom-call(f32[64,80,128]{2,1,0:T(8,128)S(1)} %get-tuple-element.8.base, f32[64,80,128]{2,1,0:T(8,128)S(1)} %get-tuple-element.9.grown, f32[2,2,80,128]{3,2,1,0:T(8,128)S(1)} %get-tuple-element.10.image, f32[2,8,128]{2,1,0:T(8,128)S(1)} %get-tuple-element.11.coef), custom_call_target="tpu_custom_call" | custom-call | tf_op jit(solution)/shard_map/combine/pallas_call | solution.py:666

commit v4 on v3

--- a/solution.py
+++ b/solution.py
@@ -458,17 +458,18 @@
         msg.start()
     smsgs = share_state(0)
     widen(1)
-    for msg in row_messages(1):
-        msg.start()
-    for c in range(2, CHUNKS):
-        widen(c)
+    widen(2)
+    widen(3)
     lax.fori_loop(0, CHUNKS, pack_corners, 0)
     for msg in corner_messages():
         msg.start()
     lax.fori_loop(0, CHUNKS, early_columns, 0)
-    for c in range(2, CHUNKS):
-        for msg in row_messages(c):
-            msg.start()
+    for msg in row_messages(1):
+        msg.start()
+    for msg in row_messages(2):
+        msg.start()
+    for msg in row_messages(3):
+        msg.start()
     squares[...] = jnp.zeros_like(squares)
     acc[...] = jnp.zeros_like(acc)
 
@@ -496,7 +497,7 @@
         sext[1, lev, inner, :] = image[0, lev, inner, :] * dext[lev, inner, :] * FILTER_SCALE
     vmsgs = share_state(1)
     acc[...] = jnp.zeros_like(acc)
-    turn_back(0, (0, 3))
+    turn_back(0, (0, 2))
     for msg in vmsgs:
         msg.wait_recv()
     turn_state(1)
@@ -542,8 +543,8 @@
             copy.wait_recv()
         return copies, jnp.sum(ref[...], axis=0)
 
-    acopies, row = gather(row, rowa, gx, n_gx, asend, arecv, lambda k: there(0, k), [(0, (3, 4)), (1, (0, 1))])
-    bcopies, row = gather(row, rowb, gy, n_gy, bsend, brecv, lambda k: there(k, 0), [(1, (1, 4))])
+    acopies, row = gather(row, rowa, gx, n_gx, asend, arecv, lambda k: there(0, k), [(0, (2, 4))])
+    bcopies, row = gather(row, rowb, gy, n_gy, bsend, brecv, lambda k: there(k, 0), [(1, (0, 4))])
 
     sums = [jnp.full((8, 128), jnp.sum(jnp.where(line == 32 * i, row, 0.0)), F32) for i in range(4)]
     bnorm_sq = sums[0] + EPS

time: 41.3 us -> 40.3 us (0.976)
  Pallas kernels: 40.5 us -> 39.6 us
    pallas_call x1, Pallas kernels: 39.1 us -> 38.1 us  [on_device(): pl.pallas_call(lambda *refs: kernel(n_gy, n_gx, *refs), name='lanczos', o...]
where the time goes in v4:
time: 40.3 us; the launch traced here: 40.2 us
  Pallas kernels  39.6 us (98%)
  between operations  0.64 us (2%)
    pallas_call x1, Pallas kernels, on_device(): pl.pallas_call(lambda *refs: kernel(n_gy, n_gx, *refs), name='lanczos', o...  38.1 us
    pallas_call x1, Pallas kernels, on_device(): pl.pallas_call(combine, name='combine', out_shape=(jax.ShapeDtypeStruct((...  1.44 us

profile of v4, /device:TPU:0, one launch (start us, length us, event | category | flops | bytes accessed | tf_op | source)
XLA Modules:
  0.0 40.2 jit_solution(12857640214727540378)
XLA Ops:
  0.6 38.1 %lanczos.1 = (f32[64,80,128]{2,1,0:T(8,128)S(1)}, f32[64,80,128]{2,1,0:T(8,128)S(1)}, f32[2,2,80,128]{3,2,1,0:T(8,128)S(1)}, f32[2,8,128]{2,1,0:T(8,128)S(1)}) custom-call(bf16[64,64,128]{2,1,0:T(8,128)(2,1)} %bitcast.2, s32[1,1,2048]{2,1,0:T(1,128)} %refs_1_.1, s32[1,1,2048]{2,1,0:T(1,128)} %refs_2_.1, f32[1,1,2048]{2,1,0:T(1,128)} %refs_3_.1, ...), custom_call_target="tpu_custom_call" | custom-call | tf_op jit(solution)/shard_map/lanczos/pallas_call | solution.py:609
  38.8 1.4 %combine.1 = (f32[64,64,128]{2,1,0:T(8,128)}, f32[2,64,128]{2,1,0:T(8,128)}) custom-call(f32[64,80,128]{2,1,0:T(8,128)S(1)} %get-tuple-element.8.base, f32[64,80,128]{2,1,0:T(8,128)S(1)} %get-tuple-element.9.grown, f32[2,2,80,128]{3,2,1,0:T(8,128)S(1)} %get-tuple-element.10.image, f32[2,8,128]{2,1,0:T(8,128)S(1)} %get-tuple-element.11.coef), custom_call_target="tpu_custom_call" | custom-call | tf_op jit(solution)/shard_map/combine/pallas_call | solution.py:667

commit v5 on v4

--- a/solution.py
+++ b/solution.py
@@ -63,7 +63,7 @@
 
 
 def sweep(load, store, masks):
-    north, south, west, east = masks
+    north, south, west, east = masks or (None,) * 4
     for first, last in ((0, NT // 2), (NT // 2, NT)):
         seen = {}
 
@@ -88,13 +88,13 @@
         def finish(r, above, here):
             for t in range(first, last):
                 out = f(r, t) + (above[t] + here[t + 1])
-                if r == 7:
+                if masks and r == 7:
                     out = out * north
-                if r == 2:
+                if masks and r == 2:
                     out = out * south
-                if t == 7:
+                if masks and t == 7:
                     out = out * west
-                if t == 10:
+                if masks and t == 10:
                     out = out * east
                 store(r, t, out)
 
@@ -432,7 +432,7 @@
         sweep(lambda r, t: column(ft, t, kind, c, r), to_work(1), masks)
         sweep(from_work(1), to_work(0), masks)
         sweep(from_work(0), to_work(1), masks)
-        sweep(from_work(1), to_image, masks)
+        sweep(from_work(1), to_image, None)
 
     def state_image(kind):
         for r in range(NR):

time: 40.3 us -> 40.3 us (level)
  no operation moved by 1% of the time
where the time goes in v5:
time: 40.3 us; the launch traced here: 40.2 us
  Pallas kernels  39.6 us (98%)
  between operations  0.64 us (2%)
    pallas_call x1, Pallas kernels, on_device(): pl.pallas_call(lambda *refs: kernel(n_gy, n_gx, *refs), name='lanczos', o...  38.1 us
    pallas_call x1, Pallas kernels, on_device(): pl.pallas_call(combine, name='combine', out_shape=(jax.ShapeDtypeStruct((...  1.44 us

profile of v5, /device:TPU:0, one launch (start us, length us, event | category | flops | bytes accessed | tf_op | source)
XLA Modules:
  0.0 40.2 jit_solution(12348194511779160685)
XLA Ops:
  0.6 38.1 %lanczos.1 = (f32[64,80,128]{2,1,0:T(8,128)S(1)}, f32[64,80,128]{2,1,0:T(8,128)S(1)}, f32[2,2,80,128]{3,2,1,0:T(8,128)S(1)}, f32[2,8,128]{2,1,0:T(8,128)S(1)}) custom-call(bf16[64,64,128]{2,1,0:T(8,128)(2,1)} %bitcast.2, s32[1,1,2048]{2,1,0:T(1,128)} %refs_1_.1, s32[1,1,2048]{2,1,0:T(1,128)} %refs_2_.1, f32[1,1,2048]{2,1,0:T(1,128)} %refs_3_.1, ...), custom_call_target="tpu_custom_call" | custom-call | tf_op jit(solution)/shard_map/lanczos/pallas_call | solution.py:609
  38.8 1.4 %combine.1 = (f32[64,64,128]{2,1,0:T(8,128)}, f32[2,64,128]{2,1,0:T(8,128)}) custom-call(f32[64,80,128]{2,1,0:T(8,128)S(1)} %get-tuple-element.8.base, f32[64,80,128]{2,1,0:T(8,128)S(1)} %get-tuple-element.9.grown, f32[2,2,80,128]{3,2,1,0:T(8,128)S(1)} %get-tuple-element.10.image, f32[2,8,128]{2,1,0:T(8,128)S(1)} %get-tuple-element.11.coef), custom_call_target="tpu_custom_call" | custom-call | tf_op jit(solution)/shard_map/combine/pallas_call | solution.py:667
